TPU v7x, 32 devices: a whole 2x2x4 slice. The times are simulated.
32 devices in a mesh: row: 8 (over z, y), col: 4 (over x, core).
Axes of the slice: x: 2, y: 2, z: 4, core: 2. Of those that a mesh axis runs over, the one named last changes fastest.
Arguments:
- moment: bfloat16 [2, 4096, 4096], P(None, 'row', 'col'), may hold values from -6 to 6
- second: float32 [2, 4096, 4096], P(None, 'row', 'col'), may hold values from 0.04 to 2
- left_old: bfloat16 [2, 4096, 4096], P(None, 'col', 'row'), may hold values from -0.09375 to 0.09375
- left_new: bfloat16 [2, 4096, 4096], P(None, 'col', 'row'), may hold values from -0.09375 to 0.09375
- right_old: bfloat16 [4096, 4096], P('row', 'col'), may hold values from -0.09375 to 0.09375
- right_new: bfloat16 [4096, 4096], P('row', 'col'), may hold values from -0.09375 to 0.09375
Outputs:
- moment_new: bfloat16 [2, 4096, 4096], P(None, 'row', 'col')
- direction: bfloat16 [2, 4096, 4096], P(None, 'row', 'col')
All inputs are finite; a program needn't handle non-finite values.
Results may differ from a plain program's by a relative error of at most 0.03.
Values may be sent and summed in bfloat16 or wider, within the bound.
A program may use at most 128 MiB of HBM per device.

v0:
```python
import jax
import jax.numpy as jnp
from jax import lax
from jax.sharding import PartitionSpec as P


def fold_stacked(left_panel, incoming):
    return jnp.einsum("bij,bjk->bik", left_panel, incoming, preferred_element_type=jnp.float32)


def fold_right(right_panel, incoming):
    return jnp.einsum("bik,qk->biq", incoming, right_panel, preferred_element_type=jnp.float32)


def local(moment, second, left_old, left_new, right_old, right_new):
    old_right_rows = lax.all_gather(right_old, "col", axis=1, tiled=True)
    right_terms = jnp.dot(right_new.T, old_right_rows, preferred_element_type=jnp.float32)
    right_panel = lax.psum(right_terms.astype(jnp.bfloat16), "row")
    old_rows = lax.all_gather(left_old, "row", axis=2, tiled=True)
    left_terms = jnp.einsum("bwi,bwj->bij", left_new, old_rows, preferred_element_type=jnp.float32)
    left_panel = lax.psum(left_terms.astype(jnp.bfloat16), "col")
    summed = fold_stacked(left_panel, lax.all_gather(moment, "row", axis=1, tiled=True))
    rotated = summed.astype(jnp.bfloat16)
    result = fold_right(right_panel, lax.all_gather(rotated, "col", axis=2, tiled=True))
    moment_new = result.astype(jnp.bfloat16)
    direction = (moment_new.astype(jnp.float32) / (jnp.sqrt(second) + 1e-08)).astype(jnp.bfloat16)
    return (moment_new, direction)


def solution(mesh):
    return jax.shard_map(
        local,
        mesh=mesh,
        in_specs=(
            P(None, "row", "col"),
            P(None, "row", "col"),
            P(None, "col", "row"),
            P(None, "col", "row"),
            P("row", "col"),
            P("row", "col"),
        ),
        out_specs=(P(None, "row", "col"), P(None, "row", "col")),
        check_vma=False,
    )
```

profile of v0, /device:TPU:0, one launch (start us, length us, event | category | flops | bytes accessed | tf_op | source)
XLA Modules:
  0.0 1013.9 jit_solution(3959504421610417472)
XLA Ops:
  7.2 0.0 copy-start
  7.2 0.0 all-gather.5.cloned.1.call-start
  7.2 0.7 all-gather.5.cloned.1.call-update
  7.9 0.0 all-gather.11.cloned.1.call-start
  8.0 0.7 all-gather.11.cloned.1.call-update
  8.7 0.0 all-gather.7.cloned.1.call-start
  8.7 0.7 all-gather.7.cloned.1.call-update
  9.4 0.0 all-reduce.3.cloned.1.call-start
  9.4 230.6 %all-gather.5.cloned.1.call-done = bf16[2,1024,4096]{2,1,0:T(8,128)(2,1)} async-done(((bf16[2,1024,512]{2,1,0:T(8,128)(2,1)}), bf16[2,1024,4096]{2,1,0:T(8,128)(2,1)}) %all-gather.5.cloned.1.call-update) | async-done | bytes 16777232 | tf_op jit(solution)/shard_map/all_gather | solution.py:19
  240.1 0.0 copy-done
  240.1 17.1 %convolution_convert_fusion.1 = bf16[2,512,4096]{2,1,0:T(8,128)(2,1)} fusion(bf16[2,1024,512]{2,1,0:T(8,128)(2,1)S(1)} %copy-done, bf16[2,1024,4096]{2,1,0:T(8,128)(2,1)} %all-gather.5.cloned.1.call-done), kind=kOutput, calls=%fused_computation.3 | convolution fusion | flops 8594128896 | bytes 27262976 | tf_op jit(solution)/shard_map/bwi,bwj->bij/dot_general | solution.py:20
  257.2 0.0 all-reduce.3.cloned.1.call-update
  257.2 0.0 all-reduce.5.cloned.1.call-start
  257.2 17.1 %all-gather.11.cloned.1.call-done = bf16[512,4096]{1,0:T(8,128)(2,1)} async-done(((bf16[512,1024]{1,0:T(8,128)(2,1)}), bf16[512,4096]{1,0:T(8,128)(2,1)}) %all-gather.11.cloned.1.call-update) | async-done | bytes 4194320 | tf_op jit(solution)/shard_map/all_gather | solution.py:16
  274.3 8.9 convolution_convert_fusion
  283.3 0.0 all-reduce.5.cloned.1.call-update
  283.3 0.2 all-gather.9.cloned.1.call-start
  283.5 220.3 %all-gather.7.cloned.1.call-done = bf16[2,4096,1024]{2,1,0:T(8,128)(2,1)} async-done(((bf16[2,512,1024]{2,1,0:T(8,128)(2,1)}), bf16[2,4096,1024]{2,1,0:T(8,128)(2,1)}) %all-gather.7.cloned.1.call-update) | async-done | bytes 16777232 | tf_op jit(solution)/shard_map/all_gather | solution.py:22
  503.8 153.4 %all-reduce.3.cloned.1.call-done = bf16[2,512,4096]{2,1,0:T(8,128)(2,1)} async-done(((bf16[2,512,4096]{2,1,0:T(8,128)(2,1)}), bf16[2,512,4096]{2,1,0:T(8,128)(2,1)}) %all-reduce.3.cloned.1.call-update) | async-done | bytes 8388624 | tf_op jit(solution)/shard_map/psum | solution.py:21
  657.2 15.8 %convolution_convert_fusion.2 = bf16[2,512,1024]{2,1,0:T(8,128)(2,1)} fusion(bf16[2,512,4096]{2,1,0:T(8,128)(2,1)} %all-reduce.3.cloned.1.call-done, bf16[2,4096,1024]{2,1,0:T(8,128)(2,1)} %all-gather.7.cloned.1.call-done), kind=kOutput, calls=%fused_computation.6 | convolution fusion | flops 8590983168 | bytes 27262976 | tf_op jit(solution)/shard_map/bij,bjk->bik/dot_general | solution.py:8
  673.0 0.0 all-gather.9.cloned.1.call-update
  673.0 258.1 %all-reduce.5.cloned.1.call-done = bf16[1024,4096]{1,0:T(8,128)(2,1)} async-done(((bf16[1024,4096]{1,0:T(8,128)(2,1)}), bf16[1024,4096]{1,0:T(8,128)(2,1)}) %all-reduce.5.cloned.1.call-update) | async-done | bytes 8388624 | tf_op jit(solution)/shard_map/psum | solution.py:18
  931.1 59.4 %all-gather.9.cloned.1.call-done = bf16[2,512,4096]{2,1,0:T(8,128)(2,1)} async-done(((bf16[2,512,1024]{2,1,0:T(8,128)(2,1)}), bf16[2,512,4096]{2,1,0:T(8,128)(2,1)}) %all-gather.9.cloned.1.call-update) | async-done | bytes 8388624 | tf_op jit(solution)/shard_map/all_gather | solution.py:24
  990.5 16.6 %divide_convert_fusion = (bf16[2,512,1024]{2,1,0:T(8,128)(2,1)}, bf16[2,512,1024]{2,1,0:T(8,128)(2,1)}) fusion(f32[2,512,1024]{2,1,0:T(8,128)} %param.7, bf16[2,512,4096]{2,1,0:T(8,128)(2,1)} %all-gather.9.cloned.1.call-done, bf16[1024,4096]{1,0:T(8,128)(2,1)} %all-reduce.5.cloned.1.call-done), kind=kOutput, calls=%fused_computation.4 | convolution fusion | flops 8595177472 | bytes 25165824 | tf_op jit(solution)/shard_map/bik,qk->biq/dot_general | solution.py:12
  (4 shorter events, 0.0 us)
Async XLA Ops:
  7.2 232.9 %copy-start = (bf16[2,1024,512]{2,1,0:T(8,128)(2,1)S(1)}, bf16[2,1024,512]{2,1,0:T(8,128)(2,1)}, u32[]{:S(2)}) copy-start(bf16[2,1024,512]{2,1,0:T(8,128)(2,1)} %param.9) | copy-start | bytes 6291460
  7.2 232.9 %all-gather.5.cloned.1.call-start = ((), (), s32[]{:S(2)}) async-start(), calls=%async_computation | async-start | bytes 18874368 | tf_op jit(solution)/shard_map/all_gather | solution.py:19
  7.9 266.4 %all-gather.11.cloned.1.call-start = ((), (), s32[]{:S(2)}) async-start(), calls=%async_computation.4 | async-start | bytes 5242880 | tf_op jit(solution)/shard_map/all_gather | solution.py:16
  8.7 495.1 %all-gather.7.cloned.1.call-start = ((), (), s32[]{:S(2)}) async-start(), calls=%async_computation.2 | async-start | bytes 18874368 | tf_op jit(solution)/shard_map/all_gather | solution.py:22
  9.4 647.8 %all-reduce.3.cloned.1.call-start = ((), (), s32[]{:S(2)}) async-start(), calls=%async_computation.1 | async-start | bytes 16777216 | tf_op jit(solution)/shard_map/psum | solution.py:21
  257.2 17.2 %copy-start.2 = (bf16[512,1024]{1,0:T(8,128)(2,1)S(1)}, bf16[512,1024]{1,0:T(8,128)(2,1)}, u32[]{:S(2)}) copy-start(bf16[512,1024]{1,0:T(8,128)(2,1)} %param.11) | copy-start | bytes 3145732
  257.2 673.9 %all-reduce.5.cloned.1.call-start = ((), (), s32[]{:S(2)}) async-start(), calls=%async_computation.5 | async-start | bytes 16777216 | tf_op jit(solution)/shard_map/psum | solution.py:18
  283.3 707.2 %all-gather.9.cloned.1.call-start = ((), (), s32[]{:S(2)}) async-start(), calls=%async_computation.3 | async-start | bytes 10485760 | tf_op jit(solution)/shard_map/all_gather | solution.py:24
  990.5 16.6 %copy-start.1 = (bf16[2,1024,512]{2,1,0:T(8,128)(2,1)S(1)}, bf16[2,1024,512]{2,1,0:T(8,128)(2,1)}, u32[]{:S(2)}) copy-start(bf16[2,1024,512]{2,1,0:T(8,128)(2,1)} %param.9) | copy-start | bytes 6291460
Sparse Core Ops, SparseCore 0:
  10.0 230.0 all-gather.4
  241.6 32.6 all-gather.10
  276.5 227.2 all-gather.6
  506.1 151.0 all-reduce.2
  660.9 270.1 all-reduce.4
  933.1 57.3 all-gather.8
where the time goes:
time: 1010 us
  waiting for transfers between devices  941 us (93%)
  matrix products  58.4 us (6%)
  between operations  14.1 us (1%)
    psum x1, waiting for transfers between devices, local(): right_panel = lax.psum(right_terms.astype(jnp.bfloat16), 'row')  258 us
    all_gather x1, waiting for transfers between devices, local(): old_rows = lax.all_gather(left_old, 'row', axis=2, tiled=True)  231 us
    all_gather x1, waiting for transfers between devices, local(): lax.all_gather(moment, 'row', axis=1, tiled=True)  220 us
    psum x1, waiting for transfers between devices, local(): left_panel = lax.psum(left_terms.astype(jnp.bfloat16), 'col')  153 us
    all_gather x1, waiting for transfers between devices, local(): lax.all_gather(rotated, 'col', axis=2, tiled=True)  59.4 us
  transfers between devices with their start and end apart: 6, of which 6 were waited for; matrix products, arithmetic and copies ran while one was open for 4% of the time, Pallas kernels for 0%

commit v1 on v0

--- a/solution.py
+++ b/solution.py
@@ -16,7 +16,15 @@
     old_right_rows = lax.all_gather(right_old, "col", axis=1, tiled=True)
     right_terms = jnp.dot(right_new.T, old_right_rows, preferred_element_type=jnp.float32)
     right_panel = lax.psum(right_terms.astype(jnp.bfloat16), "row")
-    old_rows = lax.all_gather(left_old, "row", axis=2, tiled=True)
+    n = jax.lax.axis_size("row")
+    column = [(src_i, (src_i + 1) % n) for src_i in range(n)]
+    n_now = [None] * n
+    n_now[n - 1] = left_old
+    for k0 in range(n - 2, -1, -1):
+        n_now[k0] = jax.lax.ppermute(n_now[k0 + 1], axis_name="row", perm=column)
+    y2 = jnp.concatenate(n_now, axis=2)
+    arr_out = jax.lax.axis_index("row")
+    old_rows = jnp.roll(y2, (arr_out + 1) * left_old.shape[2], axis=2)
     left_terms = jnp.einsum("bwi,bwj->bij", left_new, old_rows, preferred_element_type=jnp.float32)
     left_panel = lax.psum(left_terms.astype(jnp.bfloat16), "col")
     summed = fold_stacked(left_panel, lax.all_gather(moment, "row", axis=1, tiled=True))

time: 1010 us -> 1130 us (1.12)
  waiting for transfers between devices: 941 us -> 1020 us
  local copies, waits for them, and re-layouts: 0.02 us -> 37.2 us
    ppermute x0 -> x7, waiting for transfers between devices: none -> 333 us  [local(): n_now[k0] = jax.lax.ppermute(n_now[k0 + 1], axis_name='row', perm=column)]
    all_gather x1 -> x0, waiting for transfers between devices: 231 us -> none  [local(): old_rows = lax.all_gather(left_old, 'row', axis=2, tiled=True)]
    unnamed x6 -> x43, local copies, waits for them, and re-layouts: 0.02 us -> 35.7 us
    all_gather x1, waiting for transfers between devices: 17.1 us -> 0.02 us  [local(): old_right_rows = lax.all_gather(right_old, 'col', axis=1, tiled=True)]
    psum x1, waiting for transfers between devices: 153 us -> 138 us  [local(): left_panel = lax.psum(left_terms.astype(jnp.bfloat16), 'col')]
  transfers between devices with their start and end apart: 6 -> 12, of which waited for: 6 -> 11; matrix products, arithmetic and copies ran while one was open for 4% -> 6% of each run, Pallas kernels for 0% -> 0%
where the time goes in v1:
time: 1130 us
  waiting for transfers between devices  1020 us (90%)
  matrix products  56.5 us (5%)
  local copies, waits for them, and re-layouts  37.2 us (3%)
  between operations  13.9 us (1%)
    ppermute x7, waiting for transfers between devices, local(): n_now[k0] = jax.lax.ppermute(n_now[k0 + 1], axis_name='row', perm=column)  333 us
    psum x1, waiting for transfers between devices, local(): right_panel = lax.psum(right_terms.astype(jnp.bfloat16), 'row')  256 us
    all_gather x1, waiting for transfers between devices, local(): lax.all_gather(moment, 'row', axis=1, tiled=True)  230 us
    psum x1, waiting for transfers between devices, local(): left_panel = lax.psum(left_terms.astype(jnp.bfloat16), 'col')  138 us
    all_gather x1, waiting for transfers between devices, local(): lax.all_gather(rotated, 'col', axis=2, tiled=True)  59.4 us
    unnamed x43, local copies, waits for them, and re-layouts  35.7 us
  transfers between devices with their start and end apart: 12, of which 11 were waited for; matrix products, arithmetic and copies ran while one was open for 6% of the time, Pallas kernels for 0%

profile of v1, /device:TPU:0, one launch (start us, length us, event | category | flops | bytes accessed | tf_op | source)
XLA Modules:
  0.0 1128.4 jit_solution(14424567994983089632)
XLA Ops:
  7.2 3.0 collective-permute-start
  10.3 48.9 %collective-permute-done = bf16[2,1024,512]{2,1,0:T(8,128)(2,1)S(1)} collective-permute-done((bf16[2,1024,512]{2,1,0:T(8,128)(2,1)}, bf16[2,1024,512]{2,1,0:T(8,128)(2,1)S(1)}, u32[]{:S(2)}, u32[]{:S(2)}) %collective-permute-start) | collective-permute-done | bytes 2097184 | tf_op jit(solution)/shard_map/ppermute | solution.py:24
  60.4 49.5 %collective-permute-done.1 = bf16[2,1024,512]{2,1,0:T(8,128)(2,1)S(1)} collective-permute-done((bf16[2,1024,512]{2,1,0:T(8,128)(2,1)S(1)}, bf16[2,1024,512]{2,1,0:T(8,128)(2,1)S(1)}, u32[]{:S(2)}, u32[]{:S(2)}) %collective-permute-start.1) | collective-permute-done | bytes 2097184 | tf_op jit(solution)/shard_map/ppermute | solution.py:24
  111.3 48.6 %collective-permute-done.2 = bf16[2,1024,512]{2,1,0:T(8,128)(2,1)S(1)} collective-permute-done((bf16[2,1024,512]{2,1,0:T(8,128)(2,1)S(1)}, bf16[2,1024,512]{2,1,0:T(8,128)(2,1)S(1)}, u32[]{:S(2)}, u32[]{:S(2)}) %collective-permute-start.2) | collective-permute-done | bytes 2097184 | tf_op jit(solution)/shard_map/ppermute | solution.py:24
  161.3 47.8 %collective-permute-done.3 = bf16[2,1024,512]{2,1,0:T(8,128)(2,1)S(1)} collective-permute-done((bf16[2,1024,512]{2,1,0:T(8,128)(2,1)S(1)}, bf16[2,1024,512]{2,1,0:T(8,128)(2,1)S(1)}, u32[]{:S(2)}, u32[]{:S(2)}) %collective-permute-start.3) | collective-permute-done | bytes 2097184 | tf_op jit(solution)/shard_map/ppermute | solution.py:24
  210.4 46.9 %collective-permute-done.4 = bf16[2,1024,512]{2,1,0:T(8,128)(2,1)S(1)} collective-permute-done((bf16[2,1024,512]{2,1,0:T(8,128)(2,1)S(1)}, bf16[2,1024,512]{2,1,0:T(8,128)(2,1)S(1)}, u32[]{:S(2)}, u32[]{:S(2)}) %collective-permute-start.4) | collective-permute-done | bytes 2097184 | tf_op jit(solution)/shard_map/ppermute | solution.py:24
  258.6 46.2 %collective-permute-done.5 = bf16[2,1024,512]{2,1,0:T(8,128)(2,1)} collective-permute-done((bf16[2,1024,512]{2,1,0:T(8,128)(2,1)S(1)}, bf16[2,1024,512]{2,1,0:T(8,128)(2,1)}, u32[]{:S(2)}, u32[]{:S(2)}) %collective-permute-start.5) | collective-permute-done | bytes 2097184 | tf_op jit(solution)/shard_map/ppermute | solution.py:24
  304.9 45.4 %collective-permute-done.6 = bf16[2,1024,512]{2,1,0:T(8,128)(2,1)} collective-permute-done((bf16[2,1024,512]{2,1,0:T(8,128)(2,1)}, bf16[2,1024,512]{2,1,0:T(8,128)(2,1)}, u32[]{:S(2)}, u32[]{:S(2)}) %collective-permute-start.6) | collective-permute-done | bytes 2097184 | tf_op jit(solution)/shard_map/ppermute | solution.py:24
  350.3 3.1 constant_dynamic-update-slice_fusion.15
  353.4 3.2 constant_dynamic-update-slice_fusion.14
  356.7 1.5 constant_dynamic-update-slice_fusion.13
  358.2 1.5 constant_dynamic-update-slice_fusion.12
  361.2 1.5 constant_dynamic-update-slice_fusion.10
  364.1 1.5 constant_dynamic-update-slice_fusion.8
  365.7 3.0 constant_dynamic-update-slice_fusion.7
  368.7 3.0 constant_dynamic-update-slice_fusion.6
  380.5 14.5 %convert_bitcast_fusion = bf16[2,512,4096]{1,2,0:T(8,128)(2,1)} fusion(bf16[2,1024,512]{2,1,0:T(8,128)(2,1)S(1)} %copy-done, bf16[2,1024,8192]{2,1,0:T(8,128)(2,1)} %constant_dynamic-update-slice_fusion, s32[]{:T(128)S(6)} %select_n.14), kind=kOutput, calls=%fused_computation.4 | convolution fusion | flops 8594128896 | bytes 27262980 | tf_op jit(solution)/shard_map/bwi,bwj->bij/dot_general | solution.py:28
  396.2 9.5 convolution_convert_fusion
  405.9 138.4 %all-reduce.3.cloned.1.call-done = bf16[2,512,4096]{1,2,0:T(8,128)(2,1)} async-done(((bf16[2,512,4096]{1,2,0:T(8,128)(2,1)}), bf16[2,512,4096]{1,2,0:T(8,128)(2,1)}) %all-reduce.3.cloned.1.call-update) | async-done | bytes 8388624 | tf_op jit(solution)/shard_map/psum | solution.py:29
  544.3 229.6 %all-gather.4.cloned.1.call-done = bf16[2,4096,1024]{2,1,0:T(8,128)(2,1)} async-done(((bf16[2,512,1024]{2,1,0:T(8,128)(2,1)}), bf16[2,4096,1024]{2,1,0:T(8,128)(2,1)}) %all-gather.4.cloned.1.call-update) | async-done | bytes 16777232 | tf_op jit(solution)/shard_map/all_gather | solution.py:30
  773.9 15.9 %convolution_convert_fusion.1 = bf16[2,512,1024]{2,1,0:T(8,128)(2,1)} fusion(bf16[2,512,4096]{1,2,0:T(8,128)(2,1)} %all-reduce.3.cloned.1.call-done, bf16[2,4096,1024]{2,1,0:T(8,128)(2,1)} %all-gather.4.cloned.1.call-done), kind=kOutput, calls=%fused_computation.7 | convolution fusion | flops 8590983168 | bytes 27262976 | tf_op jit(solution)/shard_map/bij,bjk->bik/dot_general | solution.py:8
  789.8 256.0 %all-reduce.5.cloned.1.call-done = bf16[1024,4096]{1,0:T(8,128)(2,1)} async-done(((bf16[1024,4096]{1,0:T(8,128)(2,1)}), bf16[1024,4096]{1,0:T(8,128)(2,1)}) %all-reduce.5.cloned.1.call-update) | async-done | bytes 8388624 | tf_op jit(solution)/shard_map/psum | solution.py:18
  1045.9 59.4 %all-gather.6.cloned.1.call-done = bf16[2,512,4096]{2,1,0:T(8,128)(2,1)} async-done(((bf16[2,512,1024]{2,1,0:T(8,128)(2,1)}), bf16[2,512,4096]{2,1,0:T(8,128)(2,1)}) %all-gather.6.cloned.1.call-update) | async-done | bytes 8388624 | tf_op jit(solution)/shard_map/all_gather | solution.py:32
  1105.2 16.6 %divide_convert_fusion = (bf16[2,512,1024]{2,1,0:T(8,128)(2,1)}, bf16[2,512,1024]{2,1,0:T(8,128)(2,1)}) fusion(f32[2,512,1024]{2,1,0:T(8,128)} %param.7, bf16[2,512,4096]{2,1,0:T(8,128)(2,1)} %all-gather.6.cloned.1.call-done, bf16[1024,4096]{1,0:T(8,128)(2,1)} %all-reduce.5.cloned.1.call-done), kind=kOutput, calls=%fused_computation.6 | convolution fusion | flops 8595177472 | bytes 25165824 | tf_op jit(solution)/shard_map/bik,qk->biq/dot_general | solution.py:12
  (53 shorter events, 19.9 us)
Async XLA Ops:
  7.2 373.3 %copy-start = (bf16[2,1024,512]{2,1,0:T(8,128)(2,1)S(1)}, bf16[2,1024,512]{2,1,0:T(8,128)(2,1)}, u32[]{:S(2)}) copy-start(bf16[2,1024,512]{2,1,0:T(8,128)(2,1)} %param.9) | copy-start | bytes 6291460
  7.2 388.6 %all-gather.8.cloned.1.call-start = ((), (), s32[]{:S(2)}) async-start(), calls=%async_computation.3 | async-start | bytes 5242880 | tf_op jit(solution)/shard_map/all_gather | solution.py:16
  7.2 51.9 %collective-permute-start = (bf16[2,1024,512]{2,1,0:T(8,128)(2,1)}, bf16[2,1024,512]{2,1,0:T(8,128)(2,1)S(1)}, u32[]{:S(2)}, u32[]{:S(2)}) collective-permute-start(bf16[2,1024,512]{2,1,0:T(8,128)(2,1)} %param.8), channel_id=1, source_target_pairs={{0,4},{4,8},{8,12},{12,16},{16,20},{20,24},{24,28},{28,0},{1,5},{5... | collective-permute-start | bytes 6291464 | tf_op jit(solution)/shard_map/ppermute | solution.py:24
  60.4 49.5 %collective-permute-start.1 = (bf16[2,1024,512]{2,1,0:T(8,128)(2,1)S(1)}, bf16[2,1024,512]{2,1,0:T(8,128)(2,1)S(1)}, u32[]{:S(2)}, u32[]{:S(2)}) collective-permute-start(bf16[2,1024,512]{2,1,0:T(8,128)(2,1)S(1)} %collective-permute-done), channel_id=1, source_target_pairs={{0,4},{4,8},{8,12},{12,16},{16,20},{20,24},{24,28},{28,0},{1,5},{5... | collective-permute-start | bytes 6291464 | tf_op jit(solution)/shard_map/ppermute | solution.py:24
  109.9 1.4 copy-start.5
  111.3 48.6 %collective-permute-start.2 = (bf16[2,1024,512]{2,1,0:T(8,128)(2,1)S(1)}, bf16[2,1024,512]{2,1,0:T(8,128)(2,1)S(1)}, u32[]{:S(2)}, u32[]{:S(2)}) collective-permute-start(bf16[2,1024,512]{2,1,0:T(8,128)(2,1)S(1)} %collective-permute-done.1), channel_id=1, source_target_pairs={{0,4},{4,8},{8,12},{12,16},{16,20},{20,24},{24,28},{28,0},{1,5},{5... | collective-permute-start | bytes 6291464 | tf_op jit(solution)/shard_map/ppermute | solution.py:24
  159.9 1.4 copy-start.7
  161.3 47.8 %collective-permute-start.3 = (bf16[2,1024,512]{2,1,0:T(8,128)(2,1)S(1)}, bf16[2,1024,512]{2,1,0:T(8,128)(2,1)S(1)}, u32[]{:S(2)}, u32[]{:S(2)}) collective-permute-start(bf16[2,1024,512]{2,1,0:T(8,128)(2,1)S(1)} %collective-permute-done.2), channel_id=1, source_target_pairs={{0,4},{4,8},{8,12},{12,16},{16,20},{20,24},{24,28},{28,0},{1,5},{5... | collective-permute-start | bytes 6291464 | tf_op jit(solution)/shard_map/ppermute | solution.py:24
  209.1 1.3 copy-start.9
  210.4 46.9 %collective-permute-start.4 = (bf16[2,1024,512]{2,1,0:T(8,128)(2,1)S(1)}, bf16[2,1024,512]{2,1,0:T(8,128)(2,1)S(1)}, u32[]{:S(2)}, u32[]{:S(2)}) collective-permute-start(bf16[2,1024,512]{2,1,0:T(8,128)(2,1)S(1)} %collective-permute-done.3), channel_id=1, source_target_pairs={{0,4},{4,8},{8,12},{12,16},{16,20},{20,24},{24,28},{28,0},{1,5},{5... | collective-permute-start | bytes 6291464 | tf_op jit(solution)/shard_map/ppermute | solution.py:24
  257.3 1.3 copy-start.11
  258.6 46.2 %collective-permute-start.5 = (bf16[2,1024,512]{2,1,0:T(8,128)(2,1)S(1)}, bf16[2,1024,512]{2,1,0:T(8,128)(2,1)}, u32[]{:S(2)}, u32[]{:S(2)}) collective-permute-start(bf16[2,1024,512]{2,1,0:T(8,128)(2,1)S(1)} %collective-permute-done.4), channel_id=1, source_target_pairs={{0,4},{4,8},{8,12},{12,16},{16,20},{20,24},{24,28},{28,0},{1,5},{5... | collective-permute-start | bytes 6291464 | tf_op jit(solution)/shard_map/ppermute | solution.py:24
  304.8 45.5 %collective-permute-start.6 = (bf16[2,1024,512]{2,1,0:T(8,128)(2,1)}, bf16[2,1024,512]{2,1,0:T(8,128)(2,1)}, u32[]{:S(2)}, u32[]{:S(2)}) collective-permute-start(bf16[2,1024,512]{2,1,0:T(8,128)(2,1)} %collective-permute-done.5), channel_id=1, source_target_pairs={{0,4},{4,8},{8,12},{12,16},{16,20},{20,24},{24,28},{28,0},{1,5},{5... | collective-permute-start | bytes 6291464 | tf_op jit(solution)/shard_map/ppermute | solution.py:24
  304.8 239.5 %all-reduce.3.cloned.1.call-start = ((), (), s32[]{:S(2)}) async-start(), calls=%async_computation | async-start | bytes 16777216 | tf_op jit(solution)/shard_map/psum | solution.py:29
  304.9 51.8 %copy-start.12 = (bf16[2,1024,512]{2,1,0:T(8,128)(2,1)S(1)}, bf16[2,1024,512]{2,1,0:T(8,128)(2,1)}, u32[]{:S(2)}) copy-start(bf16[2,1024,512]{2,1,0:T(8,128)(2,1)} %copy-done.11) | copy-start | bytes 6291460
  304.9 53.2 %copy-start.10 = (bf16[2,1024,512]{2,1,0:T(8,128)(2,1)S(1)}, bf16[2,1024,512]{2,1,0:T(8,128)(2,1)}, u32[]{:S(2)}) copy-start(bf16[2,1024,512]{2,1,0:T(8,128)(2,1)} %copy-done.9) | copy-start | bytes 6291460
  304.9 54.8 %copy-start.8 = (bf16[2,1024,512]{2,1,0:T(8,128)(2,1)S(1)}, bf16[2,1024,512]{2,1,0:T(8,128)(2,1)}, u32[]{:S(2)}) copy-start(bf16[2,1024,512]{2,1,0:T(8,128)(2,1)} %copy-done.7) | copy-start | bytes 6291460
  353.4 7.7 copy-start.6
  356.7 6.0 copy-start.4
  358.2 6.0 copy-start.2
  395.0 378.9 %all-gather.4.cloned.1.call-start = ((), (), s32[]{:S(2)}) async-start(), calls=%async_computation.1 | async-start | bytes 18874368 | tf_op jit(solution)/shard_map/all_gather | solution.py:30
  395.7 650.1 %all-reduce.5.cloned.1.call-start = ((), (), s32[]{:S(2)}) async-start(), calls=%async_computation.4 | async-start | bytes 16777216 | tf_op jit(solution)/shard_map/psum | solution.py:18
  405.7 699.6 %all-gather.6.cloned.1.call-start = ((), (), s32[]{:S(2)}) async-start(), calls=%async_computation.2 | async-start | bytes 10485760 | tf_op jit(solution)/shard_map/all_gather | solution.py:32
  1105.2 16.6 %copy-start.1 = (bf16[2,1024,512]{2,1,0:T(8,128)(2,1)S(1)}, bf16[2,1024,512]{2,1,0:T(8,128)(2,1)}, u32[]{:S(2)}) copy-start(bf16[2,1024,512]{2,1,0:T(8,128)(2,1)} %param.9) | copy-start | bytes 6291460
  (2 other events, 2.5 us)
Sparse Core Ops, SparseCore 0:
  305.0 35.0 all-gather.7
  395.1 149.1 all-reduce.2
  546.5 227.3 all-gather.3
  777.7 268.1 all-reduce.4
  1047.8 57.3 all-gather.5
